TPU v7x, 128 devices: a whole 4x4x4 slice. The times are simulated.
128 devices in a mesh: rows: 8 (over z, core), model: 16 (over y, x).
Axes of the slice: x: 4, y: 4, z: 4, core: 2. Of those that a mesh axis runs over, the one named last changes fastest.
Arguments:
- train_query: bfloat16 [8192, 8192], P('rows', 'model'), may hold values from -0.0625 to 0.0625
- low_query: bfloat16 [8192, 16], P('rows'), may hold values from -0.0625 to 0.0625
- high_query: bfloat16 [16, 8192], P(None, 'model'), may hold values from -1.5 to 1.5
- train_key: bfloat16 [8192, 1024], P('rows', 'model'), may hold values from -0.0625 to 0.0625
- low_key: bfloat16 [8192, 16], P('rows'), may hold values from -0.0625 to 0.0625
- high_key: bfloat16 [16, 1024], P(None, 'model'), may hold values from -1.5 to 1.5
- train_value: bfloat16 [8192, 1024], P('rows', 'model'), may hold values from -0.0625 to 0.0625
- low_value: bfloat16 [8192, 16], P('rows'), may hold values from -0.0625 to 0.0625
- high_value: bfloat16 [16, 1024], P(None, 'model'), may hold values from -1.5 to 1.5
- train_mixed: bfloat16 [8192, 8192], P('model', 'rows'), may hold values from -0.0625 to 0.0625
- low_mixed: bfloat16 [8192, 16], P('model'), may hold values from -0.0625 to 0.0625
- high_mixed: bfloat16 [16, 8192], P(None, 'rows'), may hold values from -1.5 to 1.5
- norm_train: float32 [8192], P(('rows', 'model')), may hold values from 0.25 to 1.75
- norm_step: float32 [8192], P(('rows', 'model')), may hold values from -0.3 to 0.3
Outputs:
- serving_query: bfloat16 [8192, 8192], P('model')
- serving_key: bfloat16 [1024, 8192], P('model')
- serving_value: bfloat16 [1024, 8192], P('model')
- serving_mixed: bfloat16 [8192, 8192], P(None, 'model')
- serve_norm: bfloat16 [8192], replicated
All inputs are finite; a program needn't handle non-finite values.
Results may differ from a plain program's by a relative error of at most 0.001.
Values may be sent and summed in bfloat16 or wider, within the bound.
A program may use at most 128 MiB of HBM per device.

v0:
```python
import jax
import jax.numpy as jnp
from jax import lax
from jax.sharding import Mesh
from jax.sharding import PartitionSpec as P

ROWS = ("rows_0", "rows_1")
ROWS_MODEL = ("rows_0", "rows_1", "model_0", "model_1")
MODEL = ("model_0", "model_1")
mix_rate = 0.5


def turned_gather(arrays, axis, dims):
    turned = [jnp.moveaxis(a, dim, 0) for a, dim in zip(arrays, dims)]
    widths = [t[0].size for t in turned]
    both = jnp.concatenate([t.reshape(-1, w) for t, w in zip(turned, widths)], axis=1)
    out = lax.all_gather(both, axis, axis=0, tiled=True)
    parts = jnp.split(out, [sum(widths[:k]) for k in range(1, len(widths))], axis=1)
    return tuple(
        (
            jnp.moveaxis(b.reshape(-1, *t.shape[1:]), 0, dim)
            for b, t, dim in zip(parts, turned, dims)
        )
    )


def in_order(parts, dim):
    parts = jnp.moveaxis(parts, 0, dim)
    shape = parts.shape
    return parts.reshape(*shape[:dim], shape[dim] * shape[dim + 1], *shape[dim + 2 :])


def stacked_from(array, axes, order):
    parts = array
    for k in order:
        parts = lax.all_gather(parts, axes[k])
    done = order[::-1]
    back = [done.index(k) for k in range(len(axes))]
    parts = parts.transpose(*back, *range(len(axes), parts.ndim))
    return parts.reshape(-1, *array.shape)


def whole_of(array, axes, order, dim):
    return in_order(stacked_from(array, axes, order), dim)


def body(
    train_query,
    low_query,
    high_query,
    train_key,
    low_key,
    high_key,
    train_value,
    low_value,
    high_value,
    train_mixed,
    low_mixed,
    high_mixed,
    norm_train,
    norm_step,
):
    whole_query = train_query.astype(jnp.float32) + mix_rate * jnp.dot(
        low_query, high_query, preferred_element_type=jnp.float32
    )
    whole_key = train_key.astype(jnp.float32) + mix_rate * jnp.dot(
        low_key, high_key, preferred_element_type=jnp.float32
    )
    whole_value = train_value.astype(jnp.float32) + mix_rate * jnp.dot(
        low_value, high_value, preferred_element_type=jnp.float32
    )
    whole_mixed = train_mixed.astype(jnp.float32) + mix_rate * jnp.dot(
        low_mixed, high_mixed, preferred_element_type=jnp.float32
    )
    narrow_query, narrow_key, narrow_value, narrow_mixed = (
        whole_query.astype(jnp.bfloat16),
        whole_key.astype(jnp.bfloat16),
        whole_value.astype(jnp.bfloat16),
        whole_mixed.astype(jnp.bfloat16),
    )
    serving_query, serving_key, serving_value, serving_mixed = turned_gather(
        (narrow_query, narrow_key, narrow_value, narrow_mixed), ROWS, (0, 0, 0, 1)
    )
    serving_query, serving_key, serving_value, serving_mixed = (
        serving_query.T,
        serving_key.T,
        serving_value.T,
        serving_mixed.T,
    )
    serve_norm = whole_of(
        (norm_train + norm_step).astype(jnp.bfloat16), ROWS_MODEL, (0, 2, 3, 1), 0
    )
    return (serving_query, serving_key, serving_value, serving_mixed, serve_norm)


def solution(mesh):
    finer = Mesh(mesh.devices.reshape(4, 2, 4, 4), ("rows_0", "rows_1", "model_0", "model_1"))
    return jax.shard_map(
        body,
        mesh=finer,
        in_specs=(
            P(ROWS, MODEL),
            P(ROWS, None),
            P(None, MODEL),
            P(ROWS, MODEL),
            P(ROWS, None),
            P(None, MODEL),
            P(ROWS, MODEL),
            P(ROWS, None),
            P(None, MODEL),
            P(MODEL, ROWS),
            P(MODEL, None),
            P(None, ROWS),
            P(ROWS_MODEL),
            P(ROWS_MODEL),
        ),
        out_specs=(P(MODEL, None), P(MODEL, None), P(MODEL, None), P(None, MODEL), P()),
        check_vma=False,
    )
```

profile of v0, /device:TPU:1, one launch (start us, length us, event | category | flops | bytes accessed | tf_op | source)
XLA Modules:
  0.0 144.0 jit_solution(17631566383366275951)
XLA Ops:
  7.2 0.0 copy-start
  7.2 0.0 copy-start.1
  7.2 0.0 copy-start.5
  7.2 0.0 copy-start.8
  7.2 0.0 copy-start.2
  7.2 0.0 copy-start.6
  7.2 0.0 copy-start.9
  7.2 0.0 copy-start.3
  7.3 0.0 copy-start.4
  7.3 0.0 copy-start.7
  7.3 0.0 all-gather.7.cloned.1.call-start
  7.3 1.6 %copy.35 = bf16[1024,512]{0,1:T(8,128)(2,1)S(1)} copy(bf16[1024,512]{1,0:T(8,128)(2,1)} %param.14) | data formatting | bytes 2097152 | tf_op args[0]
  8.9 0.0 copy-done
  8.9 0.0 copy-done.1
  8.9 1.2 fusion
  10.1 0.0 copy-done.5
  10.1 0.0 copy-done.8
  10.1 0.0 copy-done.2
  10.1 0.2 fusion.4
  10.4 0.0 copy-done.6
  10.4 0.0 copy-done.9
  10.4 0.0 copy-done.3
  10.4 0.2 fusion.3
  10.6 0.0 copy-done.4
  10.6 0.0 copy-done.7
  10.6 0.5 add_convert_fusion.1
  11.1 1.6 %pad_maximum_fusion = bf16[1024,1152]{0,1:T(8,128)(2,1)} fusion(bf16[1024,512]{0,1:T(8,128)(2,1)S(1)} %fusion, bf16[1024,64]{0,1:T(8,128)(2,1)S(1)} %fusion.4, bf16[1024,64]{0,1:T(8,128)(2,1)S(1)} %fusion.3, bf16[1024,512]{0,1:T(8,128)(2,1)S(1)} %add_convert_fusion.1), kind=kLoop, calls=%fused_computation.1 | loop fusion | flops 9437184 | bytes 4718592 | tf_op jit(solution)/shard_map/concatenate | solution.py:16
  12.7 0.0 copy-start.12
  12.7 0.0 copy-start.10
  12.7 0.0 copy-start.11
  12.7 0.0 all-gather.7.cloned.1.call-update
  12.8 0.6 copy-done.12
  13.4 0.6 dynamic-slice
  14.6 0.0 copy-done.10
  14.6 0.0 copy-done.11
  14.7 0.2 dynamic-update-slice
  14.9 10.5 %all-reduce = bf16[256]{0:T(256)(128)(2,1)S(1)} all-reduce(bf16[256]{0:T(256)(128)(2,1)S(1)} %dynamic-update-slice), channel_id=2, replica_groups=mesh['rows_0'=4,'rows_1'=2,'model_0'=4,'model_1'=4] {'rows_0'}, use_global_device_ids=true, to_apply=%add | all-reduce | flops 256 | bytes 1024
  25.5 0.1 reshape.17
  25.5 8.4 %all-gather.4 = bf16[4,4,64]{2,1,0:T(4,128)(2,1)S(1)} all-gather(bf16[1,4,64]{2,1,0:T(4,128)(2,1)S(1)} %reshape.17), channel_id=3, replica_groups=mesh['rows_0'=4,'rows_1'=2,'model_0'=4,'model_1'=4] {'model_0'}, dimensions={0}, use_global_device_ids=true | all-gather | bytes 2560 | tf_op jit(solution)/shard_map/all_gather | solution.py:36
  33.9 10.4 %all-gather.2 = bf16[16,4,64]{2,1,0:T(4,128)(2,1)S(1)} all-gather(bf16[4,4,64]{2,1,0:T(4,128)(2,1)S(1)} %all-gather.4), channel_id=4, replica_groups=mesh['rows_0'=4,'rows_1'=2,'model_0'=4,'model_1'=4] {'model_1'}, dimensions={0}, use_global_device_ids=true | all-gather | bytes 10240 | tf_op jit(solution)/shard_map/all_gather | solution.py:36
  44.3 7.7 %all-gather.3 = bf16[8,4,4,64]{3,1,0,2:T(4,128)(2,1)S(1)} all-gather(bf16[4,4,4,64]{3,1,0,2:T(4,128)(2,1)S(1)} %bitcast.22), channel_id=5, replica_groups=mesh['rows_0'=4,'rows_1'=2,'model_0'=4,'model_1'=4] {'rows_1'}, dimensions={0}, use_global_device_ids=true | all-gather | bytes 24576 | tf_op jit(solution)/shard_map/all_gather | solution.py:36
  52.1 0.7 reshape_reshape.3
  52.8 57.7 %all-gather.7.cloned.1.call-done = bf16[8192,1152]{0,1:T(8,128)(2,1)} async-done(((bf16[1024,1152]{0,1:T(8,128)(2,1)}), bf16[8192,1152]{0,1:T(8,128)(2,1)}) %all-gather.7.cloned.1.call-update) | async-done | bytes 18874384 | tf_op jit(solution)/shard_map/all_gather | solution.py:17
  110.5 11.7 %fusion.5 = (bf16[8192,512]{0,1:T(8,128)(2,1)}, bf16[512,8192]{1,0:T(8,128)(2,1)}) fusion(bf16[8192,1152]{0,1:T(8,128)(2,1)} %all-gather.7.cloned.1.call-done), kind=kLoop, calls=%fused_computation.14 | loop fusion | bytes 33554432 | tf_op jit(solution)/shard_map/split | solution.py:18
  122.1 11.9 %copy.39 = bf16[8192,512]{1,0:T(8,128)(2,1)} copy(bf16[8192,512]{0,1:T(8,128)(2,1)} %get-tuple-element.35) | data formatting | bytes 16777216
  134.1 3.0 %slice_bitcast_fusion.1 = (bf16[64,8192]{1,0:T(8,128)(2,1)}, bf16[64,8192]{1,0:T(8,128)(2,1)}) fusion(bf16[8192,1152]{0,1:T(8,128)(2,1)} %all-gather.7.cloned.1.call-done), kind=kLoop, calls=%fused_computation.11 | loop fusion | bytes 4194304 | tf_op jit(solution)/shard_map/transpose | solution.py:87
  (5 shorter events, 0.0 us)
Async XLA Ops:
  7.2 1.7 %copy-start = (bf16[16,1024]{1,0:T(8,128)(2,1)S(1)}, bf16[16,1024]{1,0:T(8,128)(2,1)}, u32[]{:S(2)}) copy-start(bf16[16,1024]{1,0:T(8,128)(2,1)} %param.25) | copy-start | bytes 98308
  7.2 1.7 %copy-start.1 = (bf16[512,1024]{1,0:T(8,128)(2,1)S(1)}, bf16[512,1024]{1,0:T(8,128)(2,1)}, u32[]{:S(2)}) copy-start(bf16[512,1024]{1,0:T(8,128)(2,1)} %param.23) | copy-start | bytes 3145732
  7.2 2.9 %copy-start.5 = (bf16[1024,16]{0,1:T(8,128)(2,1)S(1)}, bf16[1024,16]{0,1:T(8,128)(2,1)}, u32[]{:S(2)}) copy-start(bf16[1024,16]{0,1:T(8,128)(2,1)} %param.21) | copy-start | bytes 98308
  7.2 2.9 %copy-start.8 = (bf16[16,64]{1,0:T(8,128)(2,1)S(1)}, bf16[16,64]{1,0:T(8,128)(2,1)}, u32[]{:S(2)}) copy-start(bf16[16,64]{1,0:T(8,128)(2,1)} %param.22) | copy-start | bytes 6148
  7.2 2.9 %copy-start.2 = (bf16[1024,64]{0,1:T(8,128)(2,1)S(1)}, bf16[1024,64]{0,1:T(8,128)(2,1)}, u32[]{:S(2)}) copy-start(bf16[1024,64]{0,1:T(8,128)(2,1)} %param.20) | copy-start | bytes 393220
  7.2 3.1 %copy-start.6 = (bf16[1024,16]{0,1:T(8,128)(2,1)S(1)}, bf16[1024,16]{0,1:T(8,128)(2,1)}, u32[]{:S(2)}) copy-start(bf16[1024,16]{0,1:T(8,128)(2,1)} %param.18) | copy-start | bytes 98308
  7.2 3.1 %copy-start.9 = (bf16[16,64]{1,0:T(8,128)(2,1)S(1)}, bf16[16,64]{1,0:T(8,128)(2,1)}, u32[]{:S(2)}) copy-start(bf16[16,64]{1,0:T(8,128)(2,1)} %param.19) | copy-start | bytes 6148
  7.2 3.1 %copy-start.3 = (bf16[1024,64]{0,1:T(8,128)(2,1)S(1)}, bf16[1024,64]{0,1:T(8,128)(2,1)}, u32[]{:S(2)}) copy-start(bf16[1024,64]{0,1:T(8,128)(2,1)} %param.17) | copy-start | bytes 393220
  7.3 3.4 %copy-start.4 = (bf16[1024,16]{0,1:T(8,128)(2,1)S(1)}, bf16[1024,16]{0,1:T(8,128)(2,1)}, u32[]{:S(2)}) copy-start(bf16[1024,16]{0,1:T(8,128)(2,1)} %param.15) | copy-start | bytes 98308
  7.3 3.4 %copy-start.7 = (bf16[16,512]{1,0:T(8,128)(2,1)S(1)}, bf16[16,512]{1,0:T(8,128)(2,1)}, u32[]{:S(2)}) copy-start(bf16[16,512]{1,0:T(8,128)(2,1)} %param.16) | copy-start | bytes 49156
  7.3 103.2 %all-gather.7.cloned.1.call-start = ((), (), s32[]{:S(2)}) async-start(), calls=%async_computation | async-start | bytes 21233664 | tf_op jit(solution)/shard_map/all_gather | solution.py:17
  12.7 0.7 copy-start.12
  12.7 1.9 %copy-start.10 = (f32[64]{0:T(128)S(1)}, f32[64]{0:T(128)}, u32[]{:S(2)}) copy-start(f32[64]{0:T(128)} %param.26) | copy-start | bytes 772
  12.7 1.9 %copy-start.11 = (f32[64]{0:T(128)S(1)}, f32[64]{0:T(128)}, u32[]{:S(2)}) copy-start(f32[64]{0:T(128)} %param.27) | copy-start | bytes 772
Sparse Core Ops, SparseCore 0:
  12.9 97.5 all-gather.6
where the time goes:
time: 145 us; the launch traced here: 144 us
  waiting for transfers between devices  57.7 us (40%)
  blocking collectives  37 us (26%)
  local copies, waits for them, and re-layouts  30.5 us (21%)
  between operations  14.9 us (10%)
  matrix products  2.1 us (1%)
  other arithmetic  1.62 us (1%)
    all_gather x1, waiting for transfers between devices, turned_gather(): out = lax.all_gather(both, axis, axis=0, tiled=True)  57.7 us
    all_gather x3, blocking collectives, stacked_from(): parts = lax.all_gather(parts, axes[k])  26.5 us
    unnamed x32, local copies, waits for them, and re-layouts  15.1 us
    split x1, local copies, waits for them, and re-layouts, turned_gather(): jnp.split(out, [sum(widths[:k]) for k in range(1, len(widths))], axis=1)  11.7 us
    unnamed x1, blocking collectives  10.5 us
    transpose x1, local copies, waits for them, and re-layouts, body(): serving_query, serving_key, serving_value, serving_mixed = (serving_query...  3.04 us
  transfers between devices with their start and end apart: 1, of which 1 were waited for; matrix products, arithmetic and copies ran while one was open for 1% of the time, Pallas kernels for 0%

commit v1 on v0

--- a/solution.py
+++ b/solution.py
@@ -14,7 +14,10 @@
     turned = [jnp.moveaxis(a, dim, 0) for a, dim in zip(arrays, dims)]
     widths = [t[0].size for t in turned]
     both = jnp.concatenate([t.reshape(-1, w) for t, w in zip(turned, widths)], axis=1)
-    out = lax.all_gather(both, axis, axis=0, tiled=True)
+    size = lax.axis_size(axis)
+    blocks = jnp.stack([both for _ in range(size)])
+    blocks = lax.all_to_all(blocks, axis, split_axis=0, concat_axis=0)
+    out = jnp.concatenate(blocks, axis=0)
     parts = jnp.split(out, [sum(widths[:k]) for k in range(1, len(widths))], axis=1)
     return tuple(
         (

time: 145 us -> 289 us (1.99)
  blocking collectives: 37 us -> 232 us
  waiting for transfers between devices: 57.7 us -> 0.01 us
  local copies, waits for them, and re-layouts: 30.5 us -> 45.7 us
  between operations: 14.9 us -> 1.5 us
  starting transfers between devices: 0.04 us -> 7.31 us
    unnamed x1, blocking collectives: 10.5 us -> 206 us
    all_gather x1 -> x0, waiting for transfers between devices: 57.7 us -> none  [turned_gather(): out = lax.all_gather(both, axis, axis=0, tiled=True)]
    another operation x0 -> x1, local copies, waits for them, and re-layouts: none -> 7.76 us  [turned_gather(): blocks = jnp.stack([both for _ in range(size)])]
    all_to_all x0 -> x1, starting transfers between devices: none -> 7.31 us  [turned_gather(): blocks = lax.all_to_all(blocks, axis, split_axis=0, concat_axis=0)]
    unnamed x32, local copies, waits for them, and re-layouts: 15.1 us -> 18.8 us
  transfers between devices with their start and end apart: 1 -> 1, of which waited for: 1 -> 0; matrix products, arithmetic and copies ran while one was open for 1% -> 1% of each run, Pallas kernels for 0% -> 0%
where the time goes in v1:
time: 289 us
  blocking collectives  232 us (80%)
  local copies, waits for them, and re-layouts  45.7 us (16%)
  starting transfers between devices  7.31 us (3%)
    unnamed x1, blocking collectives  206 us
    all_gather x3, blocking collectives, stacked_from(): parts = lax.all_gather(parts, axes[k])  25.7 us
    unnamed x32, local copies, waits for them, and re-layouts  18.8 us
    split x1, local copies, waits for them, and re-layouts, turned_gather(): jnp.split(out, [sum(widths[:k]) for k in range(1, len(widths))], axis=1)  11.5 us
    another operation x1, local copies, waits for them, and re-layouts, turned_gather(): blocks = jnp.stack([both for _ in range(size)])  7.76 us
    all_to_all x1, starting transfers between devices, turned_gather(): blocks = lax.all_to_all(blocks, axis, split_axis=0, concat_axis=0)  7.31 us
  transfers between devices with their start and end apart: 1, of which 0 were waited for; matrix products, arithmetic and copies ran while one was open for 1% of the time, Pallas kernels for 0%

profile of v1, /device:TPU:1, one launch (start us, length us, event | category | flops | bytes accessed | tf_op | source)
XLA Modules:
  0.0 288.8 jit_solution(1488727271037197386)
XLA Ops:
  0.6 0.0 copy-start
  0.7 0.0 copy-start.8
  0.7 0.0 copy-start.5
  0.7 0.0 copy-start.3
  0.7 0.0 copy-start.6
  0.7 0.0 copy-start.4
  0.7 0.0 copy-start.7
  0.7 0.0 copy-start.2
  0.7 1.6 copy.50
  2.4 1.2 fusion.3
  3.5 0.0 copy-done.8
  3.5 0.0 copy-done.5
  3.6 0.0 copy-done.3
  3.6 0.2 fusion.4
  3.8 0.0 copy-done
  3.8 0.0 copy-done.6
  3.8 0.5 add_convert_fusion.1
  4.3 0.0 copy-done.4
  4.3 0.0 copy-done.7
  4.3 0.0 copy-done.2
  4.3 0.5 fusion
  4.8 0.2 pad_maximum_fusion
  5.0 2.4 copy.51
  7.4 7.8 %stack.2 = bf16[8,1024,1152]{2,1,0:T(8,128)(2,1)} broadcast(bf16[1024,1152]{1,0:T(8,128)(2,1)} %copy.51), dimensions={1,2} | broadcast | bytes 21233664 | tf_op jit(solution)/shard_map/stack | solution.py:18
  15.2 0.0 copy-start.11
  15.2 0.0 copy-start.9
  15.2 0.0 copy-start.10
  15.2 7.3 %all-to-all-start = ((bf16[8,1024,1152]{2,1,0:T(8,128)(2,1)}), bf16[8,1024,1152]{2,1,0:T(8,128)(2,1)}, u32[]{:S(2)}, u32[]{:S(2)}) async-start(bf16[8,1024,1152]{2,1,0:T(8,128)(2,1)} %stack.2), calls=%async_computation | async-start | bytes 37748736 | tf_op jit(solution)/shard_map/all_to_all | solution.py:19
  22.5 0.0 copy-done.11
  22.5 0.6 dynamic-slice
  23.8 0.0 copy-done.9
  23.8 0.0 copy-done.10
  23.8 0.2 dynamic-update-slice
  24.0 206.0 %all-reduce = bf16[256]{0:T(256)(128)(2,1)S(1)} all-reduce(bf16[256]{0:T(256)(128)(2,1)S(1)} %dynamic-update-slice), channel_id=2, replica_groups=mesh['rows_0'=4,'rows_1'=2,'model_0'=4,'model_1'=4] {'rows_0'}, use_global_device_ids=true, to_apply=%add | all-reduce | flops 256 | bytes 1024
  230.1 0.1 reshape.23
  230.2 7.9 %all-gather.4 = bf16[4,4,64]{2,1,0:T(4,128)(2,1)S(1)} all-gather(bf16[1,4,64]{2,1,0:T(4,128)(2,1)S(1)} %reshape.23), channel_id=3, replica_groups=mesh['rows_0'=4,'rows_1'=2,'model_0'=4,'model_1'=4] {'model_0'}, dimensions={0}, use_global_device_ids=true | all-gather | bytes 2560 | tf_op jit(solution)/shard_map/all_gather | solution.py:39
  238.1 9.5 %all-gather.2 = bf16[16,4,64]{2,1,0:T(4,128)(2,1)S(1)} all-gather(bf16[4,4,64]{2,1,0:T(4,128)(2,1)S(1)} %all-gather.4), channel_id=4, replica_groups=mesh['rows_0'=4,'rows_1'=2,'model_0'=4,'model_1'=4] {'model_1'}, dimensions={0}, use_global_device_ids=true | all-gather | bytes 10240 | tf_op jit(solution)/shard_map/all_gather | solution.py:39
  247.6 8.3 %all-gather.3 = bf16[8,4,4,64]{3,1,0,2:T(4,128)(2,1)S(1)} all-gather(bf16[4,4,4,64]{3,1,0,2:T(4,128)(2,1)S(1)} %bitcast.23), channel_id=5, replica_groups=mesh['rows_0'=4,'rows_1'=2,'model_0'=4,'model_1'=4] {'rows_1'}, dimensions={0}, use_global_device_ids=true | all-gather | bytes 24576 | tf_op jit(solution)/shard_map/all_gather | solution.py:39
  255.9 0.7 reshape_reshape.3
  256.6 0.0 all-to-all-done
  256.6 4.4 %slice_bitcast_fusion.1 = (bf16[64,8192]{0,1:T(8,128)(2,1)}, bf16[64,8192]{0,1:T(8,128)(2,1)S(1)}) fusion(bf16[8192,1152]{1,0:T(8,128)(2,1)} %bitcast.1), kind=kLoop, calls=%fused_computation.2 | loop fusion | bytes 4194304 | tf_op jit(solution)/shard_map/transpose | solution.py:90
  261.1 11.5 %fusion.5 = (bf16[8192,512]{1,0:T(8,128)(2,1)}, bf16[512,8192]{0,1:T(8,128)(2,1)}) fusion(bf16[8192,1152]{1,0:T(8,128)(2,1)} %bitcast.1), kind=kLoop, calls=%fused_computation.14 | loop fusion | bytes 33554432 | tf_op jit(solution)/shard_map/split | solution.py:21
  272.6 2.7 copy.57
  275.3 1.6 copy.56
  276.9 0.0 copy-start.1
  276.9 11.9 %copy.55 = bf16[512,8192]{1,0:T(8,128)(2,1)} copy(bf16[512,8192]{0,1:T(8,128)(2,1)} %get-tuple-element.36) | data formatting | bytes 16777216
  288.8 0.0 copy-done.1
  (5 shorter events, 0.0 us)
Async XLA Ops:
  0.6 3.2 %copy-start = (bf16[1024,16]{0,1:T(8,128)(2,1)S(1)}, bf16[1024,16]{0,1:T(8,128)(2,1)}, u32[]{:S(2)}) copy-start(bf16[1024,16]{0,1:T(8,128)(2,1)} %param.15) | copy-start | bytes 98308
  0.7 2.9 %copy-start.8 = (bf16[16,64]{1,0:T(8,128)(2,1)S(1)}, bf16[16,64]{1,0:T(8,128)(2,1)}, u32[]{:S(2)}) copy-start(bf16[16,64]{1,0:T(8,128)(2,1)} %param.22) | copy-start | bytes 6148
  0.7 2.9 %copy-start.5 = (bf16[1024,16]{0,1:T(8,128)(2,1)S(1)}, bf16[1024,16]{0,1:T(8,128)(2,1)}, u32[]{:S(2)}) copy-start(bf16[1024,16]{0,1:T(8,128)(2,1)} %param.21) | copy-start | bytes 98308
  0.7 2.9 %copy-start.3 = (bf16[1024,64]{0,1:T(8,128)(2,1)S(1)}, bf16[1024,64]{0,1:T(8,128)(2,1)}, u32[]{:S(2)}) copy-start(bf16[1024,64]{0,1:T(8,128)(2,1)} %param.20) | copy-start | bytes 393220
  0.7 3.1 %copy-start.6 = (bf16[16,512]{1,0:T(8,128)(2,1)S(1)}, bf16[16,512]{1,0:T(8,128)(2,1)}, u32[]{:S(2)}) copy-start(bf16[16,512]{1,0:T(8,128)(2,1)} %param.16) | copy-start | bytes 49156
  0.7 3.6 %copy-start.4 = (bf16[16,1024]{1,0:T(8,128)(2,1)S(1)}, bf16[16,1024]{1,0:T(8,128)(2,1)}, u32[]{:S(2)}) copy-start(bf16[16,1024]{1,0:T(8,128)(2,1)} %param.25) | copy-start | bytes 98308
  0.7 3.6 %copy-start.7 = (bf16[512,16]{0,1:T(8,128)(2,1)S(1)}, bf16[512,16]{0,1:T(8,128)(2,1)}, u32[]{:S(2)}) copy-start(bf16[512,16]{0,1:T(8,128)(2,1)} %param.24) | copy-start | bytes 49156
  0.7 3.6 %copy-start.2 = (bf16[512,1024]{1,0:T(8,128)(2,1)S(1)}, bf16[512,1024]{1,0:T(8,128)(2,1)}, u32[]{:S(2)}) copy-start(bf16[512,1024]{1,0:T(8,128)(2,1)} %param.23) | copy-start | bytes 3145732
  15.2 7.3 %copy-start.11 = (u32[128]{0:T(128)S(1)}, u32[128]{0:T(128)}, u32[]{:S(2)}) copy-start(u32[128]{0:T(128)} %constant.8) | copy-start | bytes 1540
  15.2 8.6 %copy-start.9 = (f32[64]{0:T(128)S(1)}, f32[64]{0:T(128)}, u32[]{:S(2)}) copy-start(f32[64]{0:T(128)} %param.26) | copy-start | bytes 772
  15.2 8.6 %copy-start.10 = (f32[64]{0:T(128)S(1)}, f32[64]{0:T(128)}, u32[]{:S(2)}) copy-start(f32[64]{0:T(128)} %param.27) | copy-start | bytes 772
  15.2 241.4 %all-to-all-start = ((bf16[8,1024,1152]{2,1,0:T(8,128)(2,1)}), bf16[8,1024,1152]{2,1,0:T(8,128)(2,1)}, u32[]{:S(2)}, u32[]{:S(2)}) async-start(bf16[8,1024,1152]{2,1,0:T(8,128)(2,1)} %stack.2), calls=%async_computation | async-start | bytes 37748736 | tf_op jit(solution)/shard_map/all_to_all | solution.py:19
  276.9 11.9 %copy-start.1 = (bf16[1024,16]{0,1:T(8,128)(2,1)S(1)}, bf16[1024,16]{0,1:T(8,128)(2,1)}, u32[]{:S(2)}) copy-start(bf16[1024,16]{0,1:T(8,128)(2,1)} %param.15) | copy-start | bytes 98308
